TPU v7x, 32 devices: a whole 2x2x4 slice. The times are simulated.
32 devices in a mesh: row: 8 (over z, core), col: 4 (over y, x).
Axes of the slice: x: 2, y: 2, z: 4, core: 2. Of those that a mesh axis runs over, the one named last changes fastest.
Arguments:
- psi: bfloat16 [1024, 4096], P(('row', 'col')), may hold values from -6 to 6
- hpsi: bfloat16 [1024, 4096], P(('row', 'col')), may hold values from -0.1875 to 0.1875
- eigvec: bfloat16 [4, 8, 128, 8, 4, 128], P(None, 'row', None, None, 'col'), may hold values from -0.09375 to 0.09375
Outputs:
- correlation_tiles: float32 [4, 8, 128, 8, 4, 128], P(None, 'row', None, None, 'col')
- updated_tiles: float32 [4, 8, 128, 8, 4, 128], P(None, 'row', None, None, 'col')
- diag_part: float32 [16], replicated
- offdiag_part: float32 [16], replicated
- rotated: bfloat16 [1024, 8, 4, 128], P('row', None, 'col')
All inputs are finite; a program needn't handle non-finite values.
Results may differ from a plain program's by a relative error of at most 0.001.
Values may be sent and summed in bfloat16 or wider, within the bound.
A program may use at most 128 MiB of HBM per device.

v0:
```python
import jax
import jax.numpy as jnp
from jax import lax
from jax.sharding import PartitionSpec as P

PB = 16


def broadcast(array, axis, root):
    mine = lax.axis_index(axis) == root
    return lax.psum(jnp.where(mine, array, jnp.zeros_like(array)), axis)


def inner(left, right):
    return lax.dot_general(
        left, right, (((0,), (0,)), ((), ())), preferred_element_type=jnp.float32
    )


def on_device(psi, hpsi, eigvec):
    highest = lax.Precision.HIGHEST
    g_rows = psi.shape[0]
    bands = psi.shape[1]
    row_tiles = eigvec.shape[0]
    tile_size = eigvec.shape[2]
    col_tiles = eigvec.shape[3]
    row_count = lax.axis_size("row")
    col_count = lax.axis_size("col")
    row_id = lax.axis_index("row")
    col_id = lax.axis_index("col")
    gvecs = g_rows * row_count * col_count
    row_width = row_tiles * tile_size
    col_width = col_tiles * tile_size
    lifted = (
        psi.reshape(1, g_rows, row_tiles, row_count, tile_size),
        hpsi.reshape(1, g_rows, row_tiles, row_count, tile_size),
    )
    swapped = (
        lax.all_to_all(lifted[0], "row", split_axis=3, concat_axis=0, tiled=True),
        lax.all_to_all(lifted[1], "row", split_axis=3, concat_axis=0, tiled=True),
    )
    joined = (
        lax.all_gather(swapped[0], "col", axis=1, tiled=True),
        lax.all_gather(swapped[1], "col", axis=1, tiled=True),
    )
    psi_rows = joined[0].reshape(gvecs, row_width)
    hpsi_rows = joined[1].reshape(gvecs, row_width)
    lowered = (
        psi.reshape(g_rows, col_tiles, col_count, tile_size),
        hpsi.reshape(g_rows, col_tiles, col_count, tile_size),
    )
    moved = (
        lax.all_to_all(lowered[0], "col", split_axis=2, concat_axis=0, tiled=True),
        lax.all_to_all(lowered[1], "col", split_axis=2, concat_axis=0, tiled=True),
    )
    stacked = (
        lax.all_gather(moved[0], "row", axis=0, tiled=True),
        lax.all_gather(moved[1], "row", axis=0, tiled=True),
    )
    psi_cols = stacked[0].reshape(gvecs, col_width)
    hpsi_cols = stacked[1].reshape(gvecs, col_width)
    reduced = 0.5 * (inner(psi_rows, hpsi_cols) + inner(hpsi_rows, psi_cols))
    correlation = inner(psi_rows, psi_cols) / float(gvecs)
    blocks = reduced.reshape(row_tiles, tile_size, col_tiles, tile_size)
    leading = blocks[:, :, 0, :PB]
    shared = broadcast(leading, "col", 0)
    panel = lax.all_gather(
        shared.reshape(row_tiles, 1, tile_size, PB), "row", axis=1, tiled=True
    ).reshape(bands, PB)

    def product(vector):
        local_vec = lax.dynamic_index_in_dim(
            vector.reshape(col_tiles, col_count, tile_size), col_id, 1, keepdims=False
        )
        partial_sum = jnp.einsum("atbs,bs->at", blocks, local_vec, precision=highest)
        summed = lax.psum(partial_sum, "col")
        result = lax.all_gather(
            summed.reshape(row_tiles, 1, tile_size), "row", axis=1, tiled=True
        ).reshape(bands)
        return result

    positions = jnp.arange(bands)
    slots = jnp.arange(PB)

    def reflect(step, carry):
        vecs, images, diagonal, offdiag = carry
        column = lax.dynamic_index_in_dim(panel, step, 1, keepdims=False)
        head_v = lax.dynamic_index_in_dim(vecs, step, 0, keepdims=False)
        head_w = lax.dynamic_index_in_dim(images, step, 0, keepdims=False)
        column = (
            column
            - jnp.dot(vecs, head_w, precision=highest)
            - jnp.dot(images, head_v, precision=highest)
        )
        pivot = lax.dynamic_index_in_dim(column, step + 1, 0, keepdims=False)
        below = positions > step + 1
        tail = jnp.sum(jnp.where(below, column * column, 0.0))
        length = jnp.sqrt(pivot * pivot + tail)
        beta = jnp.where(pivot >= 0.0, -length, length)
        tau = (beta - pivot) / beta
        vector = jnp.where(
            positions == step + 1, 1.0, jnp.where(below, column / (pivot - beta), 0.0)
        )
        image = product(vector)
        image = image - jnp.dot(vecs, jnp.dot(vector, images, precision=highest), precision=highest)
        image = image - jnp.dot(images, jnp.dot(vector, vecs, precision=highest), precision=highest)
        image = tau * image
        image = image - 0.5 * tau * jnp.dot(image, vector, precision=highest) * vector
        pick = slots == step
        vecs = jnp.where(pick[None, :], vector[:, None], vecs)
        images = jnp.where(pick[None, :], image[:, None], images)
        diagonal = jnp.where(
            pick, lax.dynamic_index_in_dim(column, step, 0, keepdims=False), diagonal
        )
        offdiag = jnp.where(pick, beta, offdiag)
        return (vecs, images, diagonal, offdiag)

    start_state = (
        jnp.zeros((bands, PB), jnp.float32),
        jnp.zeros((bands, PB), jnp.float32),
        jnp.zeros((PB,), jnp.float32),
        jnp.zeros((PB,), jnp.float32),
    )
    vecs, images, diagonal, offdiag = lax.fori_loop(0, PB, reflect, start_state)

    def rows_of(matrix):
        return lax.dynamic_index_in_dim(
            matrix.reshape(row_tiles, row_count, tile_size, PB), row_id, 1, keepdims=False
        ).reshape(row_width, PB)

    def cols_of(matrix):
        return lax.dynamic_index_in_dim(
            matrix.reshape(col_tiles, col_count, tile_size, PB), col_id, 1, keepdims=False
        ).reshape(col_width, PB)

    updated = (
        reduced
        - jnp.dot(rows_of(vecs), cols_of(images).T, precision=highest)
        - jnp.dot(rows_of(images), cols_of(vecs).T, precision=highest)
    )
    flat = eigvec.reshape(row_width, col_width)
    rotated = lax.psum_scatter(
        jnp.dot(psi_rows, flat, preferred_element_type=jnp.float32),
        "row",
        scatter_dimension=0,
        tiled=True,
    )
    tile_shape = (row_tiles, 1, tile_size, col_tiles, 1, tile_size)
    return (
        correlation.reshape(tile_shape),
        updated.reshape(tile_shape),
        diagonal,
        offdiag,
        rotated.astype(jnp.bfloat16).reshape(rotated.shape[0], col_tiles, 1, tile_size),
    )


def solution(mesh):
    return jax.shard_map(
        on_device,
        mesh=mesh,
        in_specs=(
            P(("row", "col"), None),
            P(("row", "col"), None),
            P(None, "row", None, None, "col", None),
        ),
        out_specs=(
            P(None, "row", None, None, "col", None),
            P(None, "row", None, None, "col", None),
            P(),
            P(),
            P("row", None, "col", None),
        ),
        check_vma=False,
    )
```

profile of v0, /device:TPU:0, one launch (start us, length us, event | category | flops | bytes accessed | tf_op | source)
XLA Modules:
  0.0 1025.6 jit_solution(13793135316026155486)
XLA Ops:
  8.4 15.9 %all_to_all.72 = bf16[1,32,4,8,128]{4,1,2,0,3:T(8,128)(2,1)S(1)} all-to-all(bf16[1,32,4,8,128]{4,1,2,0,3:T(8,128)(2,1)S(1)} %copy.46), channel_id=1, replica_groups=mesh['row'=8,'col'=4] {'row'}, dimensions={3} | all-to-all | bytes 524288 | tf_op jit(solution)/shard_map/all_to_all | solution.py:39
  25.4 12.1 %all_to_all.73 = bf16[1,32,4,8,128]{4,1,2,0,3:T(8,128)(2,1)S(1)} all-to-all(bf16[1,32,4,8,128]{4,1,2,0,3:T(8,128)(2,1)S(1)} %copy.55), channel_id=1, replica_groups=mesh['row'=8,'col'=4] {'row'}, dimensions={3} | all-to-all | bytes 524288 | tf_op jit(solution)/shard_map/all_to_all | solution.py:40
  38.6 11.8 %all_to_all.74 = bf16[32,8,4,128]{3,1,0,2:T(8,128)(2,1)} all-to-all(bf16[32,8,4,128]{3,1,0,2:T(8,128)(2,1)S(1)} %copy.52), channel_id=1, replica_groups=mesh['row'=8,'col'=4] {'col'}, dimensions={2} | all-to-all | bytes 524288 | tf_op jit(solution)/shard_map/all_to_all | solution.py:54
  65.2 15.7 %all-gather.13.cloned.1.call-done = bf16[8,1,128,4,1,128]{5,0,4,3,1,2:T(8,128)(2,1)} async-done(((bf16[8,1,32,4,1,128]{5,0,4,3,1,2:T(8,128)(2,1)}), bf16[8,1,128,4,1,128]{5,0,4,3,1,2:T(8,128)(2,1)}) %all-gather.13.cloned.1.call-update) | async-done | bytes 1048592 | tf_op jit(solution)/shard_map/all_gather | solution.py:44
  83.8 27.9 %all-gather.9.cloned.1.call-done = bf16[1024,8,1,128]{3,1,2,0:T(8,128)(2,1)} async-done(((bf16[128,8,1,128]{3,1,2,0:T(8,128)(2,1)}), bf16[1024,8,1,128]{3,1,2,0:T(8,128)(2,1)}) %all-gather.9.cloned.1.call-update) | async-done | bytes 2097168 | tf_op jit(solution)/shard_map/all_gather | solution.py:58
  117.6 24.2 %all-gather.7.cloned.1.call-done = bf16[1024,8,1,128]{3,1,2,0:T(8,128)(2,1)} async-done(((bf16[128,8,1,128]{3,1,2,0:T(8,128)(2,1)}), bf16[1024,8,1,128]{3,1,2,0:T(8,128)(2,1)}) %all-gather.7.cloned.1.call-update) | async-done | bytes 2097168 | tf_op jit(solution)/shard_map/all_gather | solution.py:57
  152.8 16.3 %psum.21 = f32[4,1,128,16]{2,3,0,1:T(8,128)S(1)} all-reduce(f32[4,1,128,16]{2,3,0,1:T(8,128)S(1)} %select_bitcast_fusion), channel_id=1, replica_groups=mesh['row'=8,'col'=4] {'col'}, use_global_device_ids=true, to_apply=%region_0.1 | all-reduce | flops 8192 | bytes 65536 | tf_op jit(solution)/shard_map/psum | solution.py:11
  169.1 15.8 %all_gather.29 = f32[4,8,128,16]{2,3,0,1:T(8,128)S(1)} all-gather(f32[4,1,128,16]{2,3,0,1:T(8,128)S(1)} %psum.21), channel_id=1, replica_groups=mesh['row'=8,'col'=4] {'row'}, dimensions={1}, use_global_device_ids=true | all-gather | bytes 294912 | tf_op jit(solution)/shard_map/all_gather | solution.py:67
  185.2 819.2 %while.23 = (s32[]{:T(128)}, f32[4096,16]{1,0:T(8,128)}, f32[4096,16]{1,0:T(8,128)}, f32[16]{0:T(128)S(1)}, f32[16]{0:T(128)S(1)}, /*index=5*/f32[4096,16]{0,1:T...) while((s32[]{:T(128)}, f32[4096,16]{1,0:T(8,128)}, ...), condition=%wide.region_4.5_spmd.clone.clone, body=%wide.region_1.4_spmd.clone.clone.sunk | while | flops 11387518 | bytes 10909649 | solution.py:124
  210.5 12.8 %all_gather.33 = f32[4,8,128]{2,0,1:T(4,128)S(1)} all-gather(f32[4,1,128]{2,0,1:T(4,128)S(1)} %psum.25), channel_id=1, replica_groups=mesh['row'=8,'col'=4] {'row'}, dimensions={1}, use_global_device_ids=true | all-gather | bytes 18432 | tf_op jit(solution)/shard_map/while/body/eval_jaxpr/all_gather | solution.py:77
  253.1 9.1 psum.25
  262.3 12.8 %all_gather.33 = f32[4,8,128]{2,0,1:T(4,128)S(1)} all-gather(f32[4,1,128]{2,0,1:T(4,128)S(1)} %psum.25), channel_id=1, replica_groups=mesh['row'=8,'col'=4] {'row'}, dimensions={1}, use_global_device_ids=true | all-gather | bytes 18432 | tf_op jit(solution)/shard_map/while/body/eval_jaxpr/all_gather | solution.py:77
  312.8 12.8 %all_gather.33 = f32[4,8,128]{2,0,1:T(4,128)S(1)} all-gather(f32[4,1,128]{2,0,1:T(4,128)S(1)} %psum.25), channel_id=1, replica_groups=mesh['row'=8,'col'=4] {'row'}, dimensions={1}, use_global_device_ids=true | all-gather | bytes 18432 | tf_op jit(solution)/shard_map/while/body/eval_jaxpr/all_gather | solution.py:77
  355.4 9.9 psum.25
  365.3 12.8 %all_gather.33 = f32[4,8,128]{2,0,1:T(4,128)S(1)} all-gather(f32[4,1,128]{2,0,1:T(4,128)S(1)} %psum.25), channel_id=1, replica_groups=mesh['row'=8,'col'=4] {'row'}, dimensions={1}, use_global_device_ids=true | all-gather | bytes 18432 | tf_op jit(solution)/shard_map/while/body/eval_jaxpr/all_gather | solution.py:77
  415.8 12.8 %all_gather.33 = f32[4,8,128]{2,0,1:T(4,128)S(1)} all-gather(f32[4,1,128]{2,0,1:T(4,128)S(1)} %psum.25), channel_id=1, replica_groups=mesh['row'=8,'col'=4] {'row'}, dimensions={1}, use_global_device_ids=true | all-gather | bytes 18432 | tf_op jit(solution)/shard_map/while/body/eval_jaxpr/all_gather | solution.py:77
  458.5 9.1 psum.25
  467.6 12.8 %all_gather.33 = f32[4,8,128]{2,0,1:T(4,128)S(1)} all-gather(f32[4,1,128]{2,0,1:T(4,128)S(1)} %psum.25), channel_id=1, replica_groups=mesh['row'=8,'col'=4] {'row'}, dimensions={1}, use_global_device_ids=true | all-gather | bytes 18432 | tf_op jit(solution)/shard_map/while/body/eval_jaxpr/all_gather | solution.py:77
  518.1 12.8 %all_gather.33 = f32[4,8,128]{2,0,1:T(4,128)S(1)} all-gather(f32[4,1,128]{2,0,1:T(4,128)S(1)} %psum.25), channel_id=1, replica_groups=mesh['row'=8,'col'=4] {'row'}, dimensions={1}, use_global_device_ids=true | all-gather | bytes 18432 | tf_op jit(solution)/shard_map/while/body/eval_jaxpr/all_gather | solution.py:77
  560.8 9.9 psum.25
  570.6 12.8 %all_gather.33 = f32[4,8,128]{2,0,1:T(4,128)S(1)} all-gather(f32[4,1,128]{2,0,1:T(4,128)S(1)} %psum.25), channel_id=1, replica_groups=mesh['row'=8,'col'=4] {'row'}, dimensions={1}, use_global_device_ids=true | all-gather | bytes 18432 | tf_op jit(solution)/shard_map/while/body/eval_jaxpr/all_gather | solution.py:77
  621.1 12.8 %all_gather.33 = f32[4,8,128]{2,0,1:T(4,128)S(1)} all-gather(f32[4,1,128]{2,0,1:T(4,128)S(1)} %psum.25), channel_id=1, replica_groups=mesh['row'=8,'col'=4] {'row'}, dimensions={1}, use_global_device_ids=true | all-gather | bytes 18432 | tf_op jit(solution)/shard_map/while/body/eval_jaxpr/all_gather | solution.py:77
  663.8 9.1 psum.25
  672.9 12.8 %all_gather.33 = f32[4,8,128]{2,0,1:T(4,128)S(1)} all-gather(f32[4,1,128]{2,0,1:T(4,128)S(1)} %psum.25), channel_id=1, replica_groups=mesh['row'=8,'col'=4] {'row'}, dimensions={1}, use_global_device_ids=true | all-gather | bytes 18432 | tf_op jit(solution)/shard_map/while/body/eval_jaxpr/all_gather | solution.py:77
  723.4 12.8 %all_gather.33 = f32[4,8,128]{2,0,1:T(4,128)S(1)} all-gather(f32[4,1,128]{2,0,1:T(4,128)S(1)} %psum.25), channel_id=1, replica_groups=mesh['row'=8,'col'=4] {'row'}, dimensions={1}, use_global_device_ids=true | all-gather | bytes 18432 | tf_op jit(solution)/shard_map/while/body/eval_jaxpr/all_gather | solution.py:77
  766.1 9.9 psum.25
  776.0 12.8 %all_gather.33 = f32[4,8,128]{2,0,1:T(4,128)S(1)} all-gather(f32[4,1,128]{2,0,1:T(4,128)S(1)} %psum.25), channel_id=1, replica_groups=mesh['row'=8,'col'=4] {'row'}, dimensions={1}, use_global_device_ids=true | all-gather | bytes 18432 | tf_op jit(solution)/shard_map/while/body/eval_jaxpr/all_gather | solution.py:77
  826.5 12.8 %all_gather.33 = f32[4,8,128]{2,0,1:T(4,128)S(1)} all-gather(f32[4,1,128]{2,0,1:T(4,128)S(1)} %psum.25), channel_id=1, replica_groups=mesh['row'=8,'col'=4] {'row'}, dimensions={1}, use_global_device_ids=true | all-gather | bytes 18432 | tf_op jit(solution)/shard_map/while/body/eval_jaxpr/all_gather | solution.py:77
  878.3 12.8 %all_gather.33 = f32[4,8,128]{2,0,1:T(4,128)S(1)} all-gather(f32[4,1,128]{2,0,1:T(4,128)S(1)} %psum.25), channel_id=1, replica_groups=mesh['row'=8,'col'=4] {'row'}, dimensions={1}, use_global_device_ids=true | all-gather | bytes 18432 | tf_op jit(solution)/shard_map/while/body/eval_jaxpr/all_gather | solution.py:77
  928.8 12.8 %all_gather.33 = f32[4,8,128]{2,0,1:T(4,128)S(1)} all-gather(f32[4,1,128]{2,0,1:T(4,128)S(1)} %psum.25), channel_id=1, replica_groups=mesh['row'=8,'col'=4] {'row'}, dimensions={1}, use_global_device_ids=true | all-gather | bytes 18432 | tf_op jit(solution)/shard_map/while/body/eval_jaxpr/all_gather | solution.py:77
  971.5 9.9 psum.25
  981.3 12.8 %all_gather.33 = f32[4,8,128]{2,0,1:T(4,128)S(1)} all-gather(f32[4,1,128]{2,0,1:T(4,128)S(1)} %psum.25), channel_id=1, replica_groups=mesh['row'=8,'col'=4] {'row'}, dimensions={1}, use_global_device_ids=true | all-gather | bytes 18432 | tf_op jit(solution)/shard_map/while/body/eval_jaxpr/all_gather | solution.py:77
  (394 shorter events, 523.9 us)
Async XLA Ops:
  7.2 18.0 %copy-start.4 = (bf16[32,4096]{1,0:T(8,128)(2,1)S(1)}, bf16[32,4096]{1,0:T(8,128)(2,1)}, u32[]{:S(2)}) copy-start(bf16[32,4096]{1,0:T(8,128)(2,1)} %param.6) | copy-start | bytes 786436
  7.2 52.5 %all-gather.11.cloned.1.call-start = ((), (), s32[]{:S(2)}) async-start(), calls=%async_computation.8 | async-start | bytes 1310720 | tf_op jit(solution)/shard_map/all_gather | solution.py:43
  25.1 55.8 %all-gather.13.cloned.1.call-start = ((), (), s32[]{:S(2)}) async-start(), calls=%async_computation.9 | async-start | bytes 1310720 | tf_op jit(solution)/shard_map/all_gather | solution.py:44
  25.2 25.4 %copy-start.5 = (bf16[32,4096]{1,0:T(8,128)(2,1)S(1)}, bf16[32,4096]{1,0:T(8,128)(2,1)}, u32[]{:S(2)}) copy-start(bf16[32,4096]{1,0:T(8,128)(2,1)} %param.5) | copy-start | bytes 786436
  38.4 73.3 %all-gather.9.cloned.1.call-start = ((), (), s32[]{:S(2)}) async-start(), calls=%async_computation.6 | async-start | bytes 2359296 | tf_op jit(solution)/shard_map/all_gather | solution.py:58
  50.5 11.5 %copy-start.8 = (bf16[4,1,128,8,1,128]{5,3,4,2,1,0:T(8,128)(2,1)S(1)}, bf16[4,1,128,8,1,128]{5,3,4,2,1,0:T(8,128)(2,1)}, u32[]{:S(2)}) copy-start(bf16[4,1,128,8,1,128]{5,3,4,2,1,0:T(8,128)(2,1)} %param.7) | copy-start | bytes 3145732
  50.5 91.2 %all-gather.7.cloned.1.call-start = ((), (), s32[]{:S(2)}) async-start(), calls=%async_computation.5 | async-start | bytes 2359296 | tf_op jit(solution)/shard_map/all_gather | solution.py:57
  59.6 957.6 %reduce-scatter.2.cloned.1.call-start = ((), (), s32[]{:S(2)}) async-start(), calls=%async_computation.7 | async-start | bytes 4718592 | tf_op jit(solution)/shard_map/reduce_scatter | solution.py:142
  145.0 4.0 copy-start.3
  149.0 2.0 copy-start.1
  185.5 3.6 copy-start
  236.1 3.6 copy-start
  287.9 3.6 copy-start
  338.4 3.6 copy-start
  390.9 3.6 copy-start
  441.4 3.6 copy-start
  493.2 3.6 copy-start
  543.7 3.6 copy-start
  596.2 3.6 copy-start
  646.7 3.6 copy-start
  698.5 3.6 copy-start
  749.0 3.6 copy-start
  801.6 3.6 copy-start
  852.1 3.6 copy-start
  903.9 3.6 copy-start
  954.4 3.6 copy-start
  1004.4 2.9 copy-start.6
  1004.4 2.9 copy-start.7
  1010.1 3.3 copy-start.2
Sparse Core Ops, SparseCore 0:
  25.2 27.5 all-gather.10
  55.3 25.5 all-gather.12
  82.5 29.1 all-gather.8
  113.2 28.5 all-gather.6
  143.9 51.4 reduce-scatter.1
where the time goes:
time: 1030 us
  blocking collectives  423 us (41%)
  matrix products  275 us (27%)
  other arithmetic  131 us (13%)
  loops' own time  77 us (7%)
  waiting for transfers between devices  67.9 us (7%)
  local copies, waits for them, and re-layouts  36.9 us (4%)
  between operations  14.1 us (1%)
    all_gather x16, blocking collectives, product(): lax.all_gather(summed.reshape(row_tiles, 1, tile_size), 'row', axis=1, ti...  204 us
    psum x16, blocking collectives, product(): summed = lax.psum(partial_sum, 'col')  139 us
    another operation x1, loops' own time, on_device(): vecs, images, diagonal, offdiag = lax.fori_loop(0, PB, reflect, start_state)  77 us
    select_n x16, other arithmetic, reflect(): images = jnp.where(pick[None, :], image[:, None], images)  61.2 us
    while x16, matrix products  56.5 us
    dot_general x16, matrix products, reflect(): jnp.dot(images, jnp.dot(vector, vecs, precision=highest), precision=highest)  54 us
    dot_general x16, matrix products, reflect(): jnp.dot(vector, images, precision=highest)  43.2 us
    while x16, other arithmetic  37.8 us
  transfers between devices with their start and end apart: 5, of which 3 were waited for; matrix products, arithmetic and copies ran while one was open for 43% of the time, Pallas kernels for 0%

commit v1 on v0

--- a/solution.py
+++ b/solution.py
@@ -73,7 +73,10 @@
             vector.reshape(col_tiles, col_count, tile_size), col_id, 1, keepdims=False
         )
         partial_sum = jnp.einsum("atbs,bs->at", blocks, local_vec, precision=highest)
-        summed = lax.psum(partial_sum, "col")
+        size, summed = (lax.axis_size("col"), partial_sum)
+        for far in [1 << k for k in range(size.bit_length() - 1)]:
+            route = [(i, i ^ far) for i in range(size)]
+            summed = summed + lax.ppermute(summed, "col", route)
         result = lax.all_gather(
             summed.reshape(row_tiles, 1, tile_size), "row", axis=1, tiled=True
         ).reshape(bands)

time: 1030 us -> 896 us (0.87)
  blocking collectives: 423 us -> 285 us
  matrix products: 275 us -> 222 us
  waiting for transfers between devices: 67.9 us -> 102 us
  starting transfers between devices: 0.21 us -> 30.4 us
    psum x16 -> x0, blocking collectives: 139 us -> none  [product(): summed = lax.psum(partial_sum, 'col')]
    ppermute x0 -> x32, waiting for transfers between devices: none -> 34 us  [product(): summed = summed + lax.ppermute(summed, 'col', route)]
    ppermute x0 -> x32, starting transfers between devices: none -> 30.2 us  [product(): summed = summed + lax.ppermute(summed, 'col', route)]
    dot_general x16, matrix products: 43.2 us -> 17.8 us  [reflect(): jnp.dot(vector, images, precision=highest)]
    dot_general x16, matrix products: 54 us -> 28.8 us  [reflect(): jnp.dot(images, jnp.dot(vector, vecs, precision=highest), precision=highest)]
  transfers between devices with their start and end apart: 5 -> 37, of which waited for: 3 -> 19; matrix products, arithmetic and copies ran while one was open for 43% -> 43% of each run, Pallas kernels for 0% -> 0%
where the time goes in v1:
time: 896 us; the launch traced here: 894 us
  blocking collectives  285 us (32%)
  matrix products  222 us (25%)
  other arithmetic  132 us (15%)
  waiting for transfers between devices  102 us (11%)
  loops' own time  72.9 us (8%)
  local copies, waits for them, and re-layouts  36.1 us (4%)
  starting transfers between devices  30.4 us (3%)
  between operations  14.1 us (2%)
    all_gather x16, blocking collectives, product(): lax.all_gather(summed.reshape(row_tiles, 1, tile_size), 'row', axis=1, ti...  204 us
    another operation x1, loops' own time, on_device(): vecs, images, diagonal, offdiag = lax.fori_loop(0, PB, reflect, start_state)  72.9 us
    select_n x16, other arithmetic, reflect(): images = jnp.where(pick[None, :], image[:, None], images)  61.9 us
    while x16, matrix products  58.6 us
    while x16, other arithmetic  37.7 us
    ppermute x32, waiting for transfers between devices, product(): summed = summed + lax.ppermute(summed, 'col', route)  34 us
    ppermute x32, starting transfers between devices, product(): summed = summed + lax.ppermute(summed, 'col', route)  30.2 us
    dot_general x16, matrix products, reflect(): jnp.dot(vecs, jnp.dot(vector, images, precision=highest), precision=highest)  29 us
  transfers between devices with their start and end apart: 37, of which 19 were waited for; matrix products, arithmetic and copies ran while one was open for 43% of the time, Pallas kernels for 0%

profile of v1, /device:TPU:0, one launch (start us, length us, event | category | flops | bytes accessed | tf_op | source)
XLA Modules:
  0.0 894.0 jit_solution(15888798769072788288)
XLA Ops:
  8.4 15.9 %all_to_all.72 = bf16[1,32,4,8,128]{4,1,2,0,3:T(8,128)(2,1)S(1)} all-to-all(bf16[1,32,4,8,128]{4,1,2,0,3:T(8,128)(2,1)S(1)} %copy.44), channel_id=1, replica_groups=mesh['row'=8,'col'=4] {'row'}, dimensions={3} | all-to-all | bytes 524288 | tf_op jit(solution)/shard_map/all_to_all | solution.py:39
  25.4 12.1 %all_to_all.73 = bf16[1,32,4,8,128]{4,1,2,0,3:T(8,128)(2,1)S(1)} all-to-all(bf16[1,32,4,8,128]{4,1,2,0,3:T(8,128)(2,1)S(1)} %copy.53), channel_id=1, replica_groups=mesh['row'=8,'col'=4] {'row'}, dimensions={3} | all-to-all | bytes 524288 | tf_op jit(solution)/shard_map/all_to_all | solution.py:40
  38.7 11.8 %all_to_all.74 = bf16[32,8,4,128]{3,1,0,2:T(8,128)(2,1)} all-to-all(bf16[32,8,4,128]{3,1,0,2:T(8,128)(2,1)S(1)} %copy.50), channel_id=1, replica_groups=mesh['row'=8,'col'=4] {'col'}, dimensions={2} | all-to-all | bytes 524288 | tf_op jit(solution)/shard_map/all_to_all | solution.py:54
  50.8 8.8 all_to_all.75
  65.2 15.7 %all-gather.17.cloned.1.call-done = bf16[8,1,128,4,1,128]{5,0,4,3,1,2:T(8,128)(2,1)} async-done(((bf16[8,1,32,4,1,128]{5,0,4,3,1,2:T(8,128)(2,1)}), bf16[8,1,128,4,1,128]{5,0,4,3,1,2:T(8,128)(2,1)}) %all-gather.17.cloned.1.call-update) | async-done | bytes 1048592 | tf_op jit(solution)/shard_map/all_gather | solution.py:44
  83.8 27.9 %all-gather.13.cloned.1.call-done = bf16[1024,8,1,128]{3,1,2,0:T(8,128)(2,1)} async-done(((bf16[128,8,1,128]{3,1,2,0:T(8,128)(2,1)}), bf16[1024,8,1,128]{3,1,2,0:T(8,128)(2,1)}) %all-gather.13.cloned.1.call-update) | async-done | bytes 2097168 | tf_op jit(solution)/shard_map/all_gather | solution.py:58
  117.6 24.2 %all-gather.11.cloned.1.call-done = bf16[1024,8,1,128]{3,1,2,0:T(8,128)(2,1)} async-done(((bf16[128,8,1,128]{3,1,2,0:T(8,128)(2,1)}), bf16[1024,8,1,128]{3,1,2,0:T(8,128)(2,1)}) %all-gather.11.cloned.1.call-update) | async-done | bytes 2097168 | tf_op jit(solution)/shard_map/all_gather | solution.py:57
  153.2 16.3 %psum.7 = f32[4,1,128,16]{2,3,0,1:T(8,128)S(1)} all-reduce(f32[4,1,128,16]{2,3,0,1:T(8,128)S(1)} %select_bitcast_fusion), channel_id=1, replica_groups=mesh['row'=8,'col'=4] {'col'}, use_global_device_ids=true, to_apply=%region_0.1 | all-reduce | flops 8192 | bytes 65536 | tf_op jit(solution)/shard_map/psum | solution.py:11
  169.5 15.8 %all_gather.29 = f32[4,8,128,16]{2,3,0,1:T(8,128)S(1)} all-gather(f32[4,1,128,16]{2,3,0,1:T(8,128)S(1)} %psum.7), channel_id=1, replica_groups=mesh['row'=8,'col'=4] {'row'}, dimensions={1}, use_global_device_ids=true | all-gather | bytes 294912 | tf_op jit(solution)/shard_map/all_gather | solution.py:67
  185.5 691.9 %while.23 = (s32[]{:T(128)}, f32[4096,16]{1,0:T(8,128)}, f32[4096,16]{1,0:T(8,128)}, f32[16]{0:T(128)S(1)}, f32[16]{0:T(128)S(1)}, /*index=5*/f32[4096,16]{0,1:T...) while((s32[]{:T(128)}, f32[4096,16]{1,0:T(8,128)}, ...), condition=%wide.region_3.4_spmd.clone.clone, body=%wide.region_1.3_spmd.clone.clone.sunk | while | flops 11388030 | bytes 11982909 | solution.py:127
  207.8 12.8 %all-gather.5 = f32[4,1024]{1,0:T(4,128)S(1)} all-gather(f32[4,128]{1,0:T(4,128)S(1)} %add.145), channel_id=4, replica_groups=mesh['row'=8,'col'=4] {'row'}, dimensions={1}, use_global_device_ids=true | all-gather | bytes 18432 | tf_op jit(solution)/shard_map/while/body/eval_jaxpr/all_gather | solution.py:80
  221.9 3.9 broadcast_select_fusion.9
  252.2 12.8 %all-gather.5 = f32[4,1024]{1,0:T(4,128)S(1)} all-gather(f32[4,128]{1,0:T(4,128)S(1)} %add.145), channel_id=4, replica_groups=mesh['row'=8,'col'=4] {'row'}, dimensions={1}, use_global_device_ids=true | all-gather | bytes 18432 | tf_op jit(solution)/shard_map/while/body/eval_jaxpr/all_gather | solution.py:80
  266.3 3.9 broadcast_select_fusion.9
  294.6 12.8 %all-gather.5 = f32[4,1024]{1,0:T(4,128)S(1)} all-gather(f32[4,128]{1,0:T(4,128)S(1)} %add.145), channel_id=4, replica_groups=mesh['row'=8,'col'=4] {'row'}, dimensions={1}, use_global_device_ids=true | all-gather | bytes 18432 | tf_op jit(solution)/shard_map/while/body/eval_jaxpr/all_gather | solution.py:80
  308.6 3.9 broadcast_select_fusion.9
  339.0 12.8 %all-gather.5 = f32[4,1024]{1,0:T(4,128)S(1)} all-gather(f32[4,128]{1,0:T(4,128)S(1)} %add.145), channel_id=4, replica_groups=mesh['row'=8,'col'=4] {'row'}, dimensions={1}, use_global_device_ids=true | all-gather | bytes 18432 | tf_op jit(solution)/shard_map/while/body/eval_jaxpr/all_gather | solution.py:80
  353.0 3.9 broadcast_select_fusion.9
  381.3 12.8 %all-gather.5 = f32[4,1024]{1,0:T(4,128)S(1)} all-gather(f32[4,128]{1,0:T(4,128)S(1)} %add.145), channel_id=4, replica_groups=mesh['row'=8,'col'=4] {'row'}, dimensions={1}, use_global_device_ids=true | all-gather | bytes 18432 | tf_op jit(solution)/shard_map/while/body/eval_jaxpr/all_gather | solution.py:80
  395.4 3.9 broadcast_select_fusion.9
  425.7 12.8 %all-gather.5 = f32[4,1024]{1,0:T(4,128)S(1)} all-gather(f32[4,128]{1,0:T(4,128)S(1)} %add.145), channel_id=4, replica_groups=mesh['row'=8,'col'=4] {'row'}, dimensions={1}, use_global_device_ids=true | all-gather | bytes 18432 | tf_op jit(solution)/shard_map/while/body/eval_jaxpr/all_gather | solution.py:80
  439.8 3.9 broadcast_select_fusion.9
  468.1 12.8 %all-gather.5 = f32[4,1024]{1,0:T(4,128)S(1)} all-gather(f32[4,128]{1,0:T(4,128)S(1)} %add.145), channel_id=4, replica_groups=mesh['row'=8,'col'=4] {'row'}, dimensions={1}, use_global_device_ids=true | all-gather | bytes 18432 | tf_op jit(solution)/shard_map/while/body/eval_jaxpr/all_gather | solution.py:80
  512.5 12.8 %all-gather.5 = f32[4,1024]{1,0:T(4,128)S(1)} all-gather(f32[4,128]{1,0:T(4,128)S(1)} %add.145), channel_id=4, replica_groups=mesh['row'=8,'col'=4] {'row'}, dimensions={1}, use_global_device_ids=true | all-gather | bytes 18432 | tf_op jit(solution)/shard_map/while/body/eval_jaxpr/all_gather | solution.py:80
  554.9 12.8 %all-gather.5 = f32[4,1024]{1,0:T(4,128)S(1)} all-gather(f32[4,128]{1,0:T(4,128)S(1)} %add.145), channel_id=4, replica_groups=mesh['row'=8,'col'=4] {'row'}, dimensions={1}, use_global_device_ids=true | all-gather | bytes 18432 | tf_op jit(solution)/shard_map/while/body/eval_jaxpr/all_gather | solution.py:80
  599.3 12.8 %all-gather.5 = f32[4,1024]{1,0:T(4,128)S(1)} all-gather(f32[4,128]{1,0:T(4,128)S(1)} %add.145), channel_id=4, replica_groups=mesh['row'=8,'col'=4] {'row'}, dimensions={1}, use_global_device_ids=true | all-gather | bytes 18432 | tf_op jit(solution)/shard_map/while/body/eval_jaxpr/all_gather | solution.py:80
  641.6 12.8 %all-gather.5 = f32[4,1024]{1,0:T(4,128)S(1)} all-gather(f32[4,128]{1,0:T(4,128)S(1)} %add.145), channel_id=4, replica_groups=mesh['row'=8,'col'=4] {'row'}, dimensions={1}, use_global_device_ids=true | all-gather | bytes 18432 | tf_op jit(solution)/shard_map/while/body/eval_jaxpr/all_gather | solution.py:80
  686.0 12.8 %all-gather.5 = f32[4,1024]{1,0:T(4,128)S(1)} all-gather(f32[4,128]{1,0:T(4,128)S(1)} %add.145), channel_id=4, replica_groups=mesh['row'=8,'col'=4] {'row'}, dimensions={1}, use_global_device_ids=true | all-gather | bytes 18432 | tf_op jit(solution)/shard_map/while/body/eval_jaxpr/all_gather | solution.py:80
  728.4 12.8 %all-gather.5 = f32[4,1024]{1,0:T(4,128)S(1)} all-gather(f32[4,128]{1,0:T(4,128)S(1)} %add.145), channel_id=4, replica_groups=mesh['row'=8,'col'=4] {'row'}, dimensions={1}, use_global_device_ids=true | all-gather | bytes 18432 | tf_op jit(solution)/shard_map/while/body/eval_jaxpr/all_gather | solution.py:80
  772.8 12.8 %all-gather.5 = f32[4,1024]{1,0:T(4,128)S(1)} all-gather(f32[4,128]{1,0:T(4,128)S(1)} %add.145), channel_id=4, replica_groups=mesh['row'=8,'col'=4] {'row'}, dimensions={1}, use_global_device_ids=true | all-gather | bytes 18432 | tf_op jit(solution)/shard_map/while/body/eval_jaxpr/all_gather | solution.py:80
  815.1 12.8 %all-gather.5 = f32[4,1024]{1,0:T(4,128)S(1)} all-gather(f32[4,128]{1,0:T(4,128)S(1)} %add.145), channel_id=4, replica_groups=mesh['row'=8,'col'=4] {'row'}, dimensions={1}, use_global_device_ids=true | all-gather | bytes 18432 | tf_op jit(solution)/shard_map/while/body/eval_jaxpr/all_gather | solution.py:80
  859.5 12.8 %all-gather.5 = f32[4,1024]{1,0:T(4,128)S(1)} all-gather(f32[4,128]{1,0:T(4,128)S(1)} %add.145), channel_id=4, replica_groups=mesh['row'=8,'col'=4] {'row'}, dimensions={1}, use_global_device_ids=true | all-gather | bytes 18432 | tf_op jit(solution)/shard_map/while/body/eval_jaxpr/all_gather | solution.py:80
  (510 shorter events, 431.2 us)
Async XLA Ops:
  7.2 52.6 %all-gather.15.cloned.1.call-start = ((), (), s32[]{:S(2)}) async-start(), calls=%async_computation.8 | async-start | bytes 1310720 | tf_op jit(solution)/shard_map/all_gather | solution.py:43
  25.1 55.8 %all-gather.17.cloned.1.call-start = ((), (), s32[]{:S(2)}) async-start(), calls=%async_computation.9 | async-start | bytes 1310720 | tf_op jit(solution)/shard_map/all_gather | solution.py:44
  38.4 73.3 %all-gather.13.cloned.1.call-start = ((), (), s32[]{:S(2)}) async-start(), calls=%async_computation.6 | async-start | bytes 2359296 | tf_op jit(solution)/shard_map/all_gather | solution.py:58
  50.5 91.2 %all-gather.11.cloned.1.call-start = ((), (), s32[]{:S(2)}) async-start(), calls=%async_computation.5 | async-start | bytes 2359296 | tf_op jit(solution)/shard_map/all_gather | solution.py:57
  59.6 826.0 %reduce-scatter.2.cloned.1.call-start = ((), (), s32[]{:S(2)}) async-start(), calls=%async_computation.7 | async-start | bytes 4718592 | tf_op jit(solution)/shard_map/reduce_scatter | solution.py:145
  197.6 6.6 collective-permute-start
  204.2 3.7 collective-permute-start.1
  239.9 8.6 collective-permute-start
  248.6 3.7 collective-permute-start.1
  284.3 6.6 collective-permute-start
  290.9 3.7 collective-permute-start.1
  326.7 8.6 collective-permute-start
  335.3 3.7 collective-permute-start.1
  371.1 6.6 collective-permute-start
  377.7 3.7 collective-permute-start.1
  413.5 8.6 collective-permute-start
  422.1 3.7 collective-permute-start.1
  457.9 6.6 collective-permute-start
  464.5 3.7 collective-permute-start.1
  500.2 8.6 collective-permute-start
  508.8 3.7 collective-permute-start.1
  544.6 6.6 collective-permute-start
  551.2 3.7 collective-permute-start.1
  587.0 8.6 collective-permute-start
  631.4 6.6 collective-permute-start
  673.7 8.6 collective-permute-start
  682.4 3.7 collective-permute-start.1
  718.1 6.6 collective-permute-start
  724.7 3.7 collective-permute-start.1
  760.5 8.6 collective-permute-start
  804.9 6.6 collective-permute-start
  847.3 8.6 collective-permute-start
  (47 other events, 196.8 us)
Sparse Core Ops, SparseCore 0:
  25.2 27.5 all-gather.14
  55.3 25.5 all-gather.16
  82.5 29.1 all-gather.12
  113.2 28.5 all-gather.10
  143.9 51.4 reduce-scatter.1
